TPU v7x, 256 devices: a whole 4x4x8 slice. The times are simulated.
256 devices in a mesh: dp: 64 (over z, y, core), mp: 4 (over x).
Axes of the slice: x: 4, y: 4, z: 8, core: 2. Of those that a mesh axis runs over, the one named last changes fastest.
Arguments:
- tokens: bfloat16 [393216, 512], P('dp'), may hold values from -6 to 6
- w_uvqk: bfloat16 [512, 2048], P(None, 'mp')
- w_out: bfloat16 [512, 512], replicated, may hold values from -0.25 to 0.25
- hist_len: int32 [64, 24], P('dp'), may hold values from 64 to 256, as said below
- owner: int32 [64, 24], P('dp'), may hold values from 0 to 63, as said below
- recv_offset: int32 [64, 24], P('dp'), may hold values from 0 to 47, as said below
- block_start: int32 [64, 24], P('dp'), may hold values from 0 to 47, as said below
Outputs:
- packed_out: bfloat16 [393216, 512], P('dp', 'mp')
- user_state: bfloat16 [1536, 512], P('dp', 'mp')
Inputs may be any that keep to these rules, and one draw needn't show every extreme that they name: User (d, u) has ceil(hist_len / 128) blocks, at most 2. owner[d, u] = (p(d) + r(u mod 64)) mod 64 for two permutations p, r of the indices of dp drawn from the seed: every owner receives exactly 24 users, and one device sends at most 1 users to one owner. On some owner every received user has 2 blocks. `recv_offset`: the users of one owner occupy disjoint runs of its 48 blocks, in the order of u; on some owner they fill all 48 blocks. `block_start`: the users of one device occupy disjoint runs of its 48 blocks, in the order of u.
All inputs are finite; a program needn't handle non-finite values.
Results may differ from a plain program's by a relative error of at most 0.0059.
Values may be sent and summed in bfloat16 or wider, within the bound.
A program may use at most 128 MiB of HBM per device.

v0:
```python
import jax
import jax.numpy as jnp
from jax import lax
from jax.sharding import PartitionSpec as P

D = 512
HEADS = 4
BLOCK = 128
MAXB = 2
BLK_DEV = 48
EPS = 1e-05


def sent_to_all(shard, axis):
    count = lax.axis_size(axis)
    return lax.all_to_all(
        jnp.broadcast_to(shard[None], (count, *shard.shape)), axis, 0, 0, tiled=True
    )


def over_copies(shard, axis):
    everything = sent_to_all(shard, axis)
    return jnp.sum(everything, axis=0)


def together(arrays, axis):
    ends = [0]
    for a in arrays:
        ends.append(ends[-1] + a.size)
    subtotal = over_copies(jnp.concatenate([a.ravel() for a in arrays]), axis)
    return tuple((subtotal[b:e].reshape(a.shape) for a, b, e in zip(arrays, ends, ends[1:])))


def in_one_piece(arrays, axis, dim, along):
    widths = [a.shape[along] for a in arrays]
    both = jnp.concatenate(arrays, axis=along)
    result = lax.all_gather(both, axis, axis=dim, tiled=True)
    return tuple(jnp.split(result, [sum(widths[:k]) for k in range(1, len(widths))], axis=along))


def norm_rows(values):
    average = jnp.mean(values, axis=-1, keepdims=True)
    variance = jnp.mean(values * values, axis=-1, keepdims=True) - average * average
    return (values - average) * lax.rsqrt(variance + EPS)


def attend(query, keys, values, query_user, key_user):
    row_count, head_size = query.shape
    tile_rows = 4 * BLOCK
    back_rows = (MAXB - 1) * BLOCK
    scaling = (D // HEADS) ** (-0.5)
    keys_ext = jnp.concatenate([jnp.zeros((back_rows, head_size), keys.dtype), keys], 0)
    values_ext = jnp.concatenate([jnp.zeros((back_rows, head_size), values.dtype), values], 0)
    users_ext = jnp.concatenate([jnp.full((back_rows,), -2, jnp.int32), key_user], 0)
    query_pos = jnp.arange(tile_rows, dtype=jnp.int32)[:, None] + back_rows
    key_pos = jnp.arange(tile_rows + back_rows, dtype=jnp.int32)[None, :]

    def one_tile(start):
        query_tile = lax.dynamic_slice_in_dim(query, start, tile_rows, 0)
        key_tile = lax.dynamic_slice_in_dim(keys_ext, start, tile_rows + back_rows, 0)
        value_tile = lax.dynamic_slice_in_dim(values_ext, start, tile_rows + back_rows, 0)
        query_owner = lax.dynamic_slice_in_dim(query_user, start, tile_rows, 0)
        key_owner = lax.dynamic_slice_in_dim(users_ext, start, tile_rows + back_rows, 0)
        raw_scores = (
            lax.dot_general(
                query_tile, key_tile, (((1,), (1,)), ((), ())), preferred_element_type=jnp.float32
            )
            * scaling
        )
        allowed = (query_owner[:, None] == key_owner[None, :]) & (key_pos <= query_pos)
        weights = jnp.where(allowed, jax.nn.silu(raw_scores) / (MAXB * BLOCK), 0.0).astype(
            jnp.bfloat16
        )
        return jnp.dot(weights, value_tile, preferred_element_type=jnp.float32)

    tile_starts = jnp.arange(row_count // tile_rows, dtype=jnp.int32) * tile_rows
    return lax.map(one_tile, tile_starts).reshape(row_count, head_size)


def layer_rows(rows_in, query_user, key_user, w_uvqk, w_out):
    row_count = rows_in.shape[0]
    head_size = D // HEADS
    mp_size = lax.axis_size("mp")
    portion = lax.axis_index("mp")
    quarter = D // mp_size
    local_heads = w_uvqk.shape[1] // (4 * head_size)
    widened = rows_in.astype(jnp.float32)
    normed = norm_rows(widened).astype(jnp.bfloat16)
    projected = jax.nn.silu(jnp.dot(normed, w_uvqk, preferred_element_type=jnp.float32)).astype(
        jnp.bfloat16
    )
    pieces = projected.reshape(row_count, local_heads, 4, head_size)
    outputs = attend(pieces[:, 0, 2], pieces[:, 0, 3], pieces[:, 0, 1], query_user, key_user)
    totals = together((jnp.sum(outputs, 1), jnp.sum(outputs * outputs, 1)), "mp")
    average = totals[0] / D
    variance = totals[1] / D - average * average
    gates = pieces[:, :, 0].reshape(row_count, local_heads * head_size).astype(jnp.float32)
    gated_rows = ((outputs - average[:, None]) * lax.rsqrt(variance + EPS)[:, None] * gates).astype(
        jnp.bfloat16
    )
    every_head = lax.all_gather(gated_rows, "mp", axis=1, tiled=True)
    out_columns = lax.dynamic_slice_in_dim(w_out, portion * quarter, quarter, 1)
    mixed_rows = jnp.dot(every_head, out_columns, preferred_element_type=jnp.float32)
    residual = lax.dynamic_slice_in_dim(widened, portion * quarter, quarter, 1)
    return (mixed_rows + residual).astype(jnp.bfloat16)


def row_labels(block_user, block_fill):
    in_block = jnp.arange(BLOCK, dtype=jnp.int32)[None, :]
    row_live = (in_block < block_fill[:, None]).reshape(-1)
    row_user = jnp.broadcast_to(block_user[:, None], (block_user.shape[0], BLOCK)).reshape(-1)
    return (row_live, jnp.where(row_live, row_user, -3), jnp.where(row_live, row_user, -2))


def per_device(tokens, w_uvqk, w_out, hist_len, owner, recv_offset, block_start):
    dp_size = lax.axis_size("dp")
    mp_size = lax.axis_size("mp")
    myself = lax.axis_index("dp")
    user_count = hist_len.shape[1]
    per_pair = -(-user_count // dp_size)
    pair_cap = per_pair * MAXB
    quarter = D // mp_size
    lengths = hist_len[0]
    owners = owner[0]
    starts = block_start[0]
    counts = (lengths + BLOCK - 1) // BLOCK
    user_ids = jnp.arange(user_count, dtype=jnp.int32)
    earlier = user_ids[None, :] < user_ids[:, None]
    same_owner = (owners[:, None] == owners[None, :]) & earlier
    in_pair = jnp.sum(jnp.where(same_owner, counts[None, :], 0), axis=1)
    slot_ids = jnp.arange(pair_cap, dtype=jnp.int32)
    device_ids = jnp.arange(dp_size, dtype=jnp.int32)
    slot_step = slot_ids[None, :, None] - in_pair[None, None, :]
    sending = (
        (owners[None, None, :] == device_ids[:, None, None])
        & (slot_step >= 0)
        & (slot_step < counts[None, None, :])
    )
    send_block = jnp.sum(jnp.where(sending, starts[None, None, :] + slot_step, 0), axis=2)
    all_len, all_owner, all_offset = in_one_piece((hist_len, owner, recv_offset), "dp", 0, 1)
    all_counts = (all_len + BLOCK - 1) // BLOCK
    all_before = (all_owner[:, :, None] == all_owner[:, None, :]) & earlier[None]
    all_in_pair = jnp.sum(jnp.where(all_before, all_counts[:, None, :], 0), axis=2)
    owned = all_owner == myself
    flat_owned = owned.reshape(-1)
    flat_len = all_len.reshape(-1)
    flat_offset = all_offset.reshape(-1)
    flat_counts = all_counts.reshape(-1)
    flat_in_pair = all_in_pair.reshape(-1)
    candidate_ids = jnp.arange(dp_size * user_count, dtype=jnp.int32)
    source_ids = candidate_ids // user_count
    block_ids = jnp.arange(BLK_DEV, dtype=jnp.int32)
    land_step = block_ids[:, None] - flat_offset[None, :]
    landed = flat_owned[None, :] & (land_step >= 0) & (land_step < flat_counts[None, :])
    slot_index = jnp.sum(
        jnp.where(landed, source_ids[None, :] * pair_cap + flat_in_pair[None, :] + land_step, 0),
        axis=1,
    )
    owned_user = jnp.sum(jnp.where(landed, candidate_ids[None, :], 0), axis=1)
    owned_fill = jnp.sum(
        jnp.where(landed, jnp.clip(flat_len[None, :] - land_step * BLOCK, 0, BLOCK), 0), axis=1
    )
    owned_live, owned_query, owned_key = row_labels(owned_user, owned_fill)
    local_step = block_ids[:, None] - starts[None, :]
    within = (local_step >= 0) & (local_step < counts[None, :])
    local_user = jnp.sum(jnp.where(within, user_ids[None, :], 0), axis=1)
    local_fill = jnp.sum(
        jnp.where(within, jnp.clip(lengths[None, :] - local_step * BLOCK, 0, BLOCK), 0), axis=1
    )
    local_live, local_query, local_key = row_labels(local_user, local_fill)
    results = layer_rows(tokens, local_query, local_key, w_uvqk, w_out)
    state = jnp.take(results, starts * BLOCK + lengths - 1, axis=0)
    outgoing = jnp.take(results.reshape(BLK_DEV, BLOCK, quarter), send_block, axis=0)
    arrived = lax.all_to_all(outgoing, "dp", split_axis=0, concat_axis=0, tiled=True)
    gathered = jnp.take(
        arrived.reshape(dp_size * pair_cap, BLOCK, quarter), slot_index, axis=0
    ).reshape(BLK_DEV * BLOCK, quarter)
    packed = jnp.where(owned_live[:, None], gathered, jnp.zeros_like(gathered))
    return (packed, state)


def solution(mesh):
    in_specs = (
        P("dp", None),
        P(None, "mp"),
        P(),
        P("dp", None),
        P("dp", None),
        P("dp", None),
        P("dp", None),
    )
    out_specs = (P("dp", "mp"), P("dp", "mp"))
    return jax.shard_map(
        per_device, mesh=mesh, in_specs=in_specs, out_specs=out_specs, check_vma=False
    )
```

profile of v0, /device:TPU:1, one launch (start us, length us, event | category | flops | bytes accessed | tf_op | source)
XLA Modules:
  0.0 370.8 jit_solution(17628559279992237693)
XLA Ops:
  7.2 4.8 %convert_reduce_fusion = (f32[6144]{0:T(1024)S(1)}, f32[6144]{0:T(1024)S(1)}) fusion(bf16[6144,512]{1,0:T(8,128)(2,1)} %param.9), kind=kLoop, calls=%fused_computation.31 | loop fusion | flops 12570624 | bytes 6340608 | tf_op jit(solution)/shard_map/reduce_sum | solution.py:42
  12.0 8.0 %multiply_convert_fusion = bf16[6144,512]{0,1:T(8,128)(2,1)S(1)} fusion(bf16[512,512]{1,0:T(8,128)(2,1)S(1)} %copy-done, bf16[6144,512]{1,0:T(8,128)(2,1)S(1)} %copy-done.2, f32[6144]{0:T(1024)S(1)} %get-tuple-element.108, f32[6144]{0:T(1024)S(1)} %get-tuple-element.107), kind=kOutput, calls=%fused_computation.28 | convolution fusion | flops 3249537024 | bytes 13156352 | tf_op jit(solution)/shard_map/dot_general | solution.py:89
  20.0 2.3 fusion.59
  22.3 1.3 copy-done.3
  23.7 2.6 copy.50
  26.3 2.6 copy.51
  28.9 2.8 concatenate.17
  31.7 1.3 concatenate.18
  33.0 1.6 copy.49
  34.7 78.6 %while.11 = (s32[]{:T(128)}, f32[12,512,128]{2,1,0:T(8,128)}, s32[12]{0:T(128)S(1)}, s32[6144]{0:T(1024)S(1)}, s32[6272]{0:T(1024)S(1)}, /*index=5*/bf16[6144,12...) while((s32[]{:T(128)}, f32[12,512,128]{2,1,0:T(8,128)}, ...), condition=%wide.region_10.11_spmd.clone, body=%wide.region_9.10_spmd.clone.sunk | while | flops 171377152 | bytes 741060 | solution.py:77
  34.8 0.6 dynamic_slice.53
  38.7 2.6 fusion.70
  41.3 0.6 dynamic_slice.53
  45.3 2.6 fusion.70
  47.9 0.6 dynamic_slice.53
  51.8 2.6 fusion.70
  54.4 0.6 dynamic_slice.53
  58.4 2.6 fusion.70
  61.0 0.6 dynamic_slice.53
  64.9 2.6 fusion.70
  67.5 0.6 dynamic_slice.53
  71.5 2.6 fusion.70
  74.1 0.6 dynamic_slice.53
  78.0 2.6 fusion.70
  80.6 0.6 dynamic_slice.53
  84.5 2.6 fusion.70
  87.2 0.6 dynamic_slice.53
  91.1 2.6 fusion.70
  93.7 0.6 dynamic_slice.53
  97.7 2.6 fusion.70
  104.2 2.6 fusion.70
  110.8 2.6 fusion.70
  113.4 3.6 fusion.58
  117.0 0.8 broadcast_in_dim.174
  117.8 4.8 %all-to-all-start = ((f32[4,1,12288]{2,1,0:T(1,128)}), f32[4,1,12288]{2,1,0:T(1,128)S(1)}, u32[]{:S(2)}, u32[]{:S(2)}) async-start(f32[4,1,12288]{2,1,0:T(1,128)} %broadcast_in_dim.174), calls=%async_computation | async-start | bytes 393216 | tf_op jit(solution)/shard_map/all_to_all | solution.py:16
  122.6 3.5 copy.46
  126.2 1.6 all-to-all-done
  128.0 4.0 %fusion.30 = bf16[6144,128]{0,1:T(8,128)(2,1)} fusion(f32[6144,128]{0,1:T(8,128)} %copy.46, bf16[6144,1,4,128]{0,3,2,1:T(8,128)(2,1)} %bitcast.68, f32[6144]{0:T(1024)S(1)} %get-tuple-element.102, f32[6144]{0:T(1024)S(1)} %get-tuple-element.101), kind=kLoop, calls=%fused_computation.39 | loop fusion | flops 3932160 | bytes 6340608 | tf_op jit(solution)/shard_map/convert_element_type | solution.py:98
  132.0 9.2 %convert_element_type.24 = f32[6144,512]{1,0:T(8,128)} convert(bf16[6144,512]{1,0:T(8,128)(2,1)} %param.9) | non-fusion elementwise | flops 3145728 | bytes 18874368 | tf_op jit(solution)/shard_map/convert_element_type | solution.py:87
  142.0 60.7 %all-gather.3.cloned.1.call-done = bf16[6144,512]{0,1:T(8,128)(2,1)} async-done(((bf16[6144,128]{0,1:T(8,128)(2,1)}), bf16[6144,512]{0,1:T(8,128)(2,1)}) %all-gather.3.cloned.1.call-update) | async-done | bytes 6291472 | tf_op jit(solution)/shard_map/all_gather | solution.py:101
  202.7 5.6 %fusion.26 = bf16[6144,128]{1,0:T(8,128)(2,1)S(1)} fusion(bf16[6144,512]{0,1:T(8,128)(2,1)} %all-gather.3.cloned.1.call-done, f32[6144,512]{1,0:T(8,128)} %convert_element_type.24, s32[]{:T(128)S(6)} %select_n.164, bf16[512,512]{1,0:T(8,128)(2,1)} %param.11), kind=kOutput, calls=%fused_computation.33 | convolution fusion | flops 806879232 | bytes 11142144 | tf_op jit(solution)/shard_map/dot_general | solution.py:103
  208.4 3.1 gather_fusion
  211.4 4.6 %broadcast_select_fusion = bf16[64,2,128,128]{3,2,1,0:T(8,128)(2,1)} fusion(bf16[64,2,128,128]{3,2,1,0:T(8,128)(2,1)} %bitcast.65, pred[64,2]{1,0:T(8,128)(4,1)S(1)} %copy.41), kind=kLoop, calls=%fused_computation.37 | loop fusion | flops 2097152 | bytes 8388736 | tf_op jit(solution)/shard_map/jit(_take)/select_n | solution.py:173
  216.0 11.2 %all-to-all-start.1 = ((bf16[64,2,128,128]{3,2,1,0:T(8,128)(2,1)}), bf16[64,2,128,128]{3,2,1,0:T(8,128)(2,1)}, u32[]{:S(2)}, u32[]{:S(2)}) async-start(bf16[64,2,128,128]{3,2,1,0:T(8,128)(2,1)} %broadcast_select_fusion), calls=%async_computation.1 | async-start | bytes 8388608 | tf_op jit(solution)/shard_map/all_to_all | solution.py:174
  227.3 125.6 %all-gather = s32[64,1,72]{2,1,0:T(1,128)S(1)} all-gather(s32[1,1,72]{2,1,0:T(1,128)S(1)} %add_bitcast_fusion), channel_id=1, replica_groups=mesh['dp'=64,'mp'=4] {'dp'}, dimensions={0}, use_global_device_ids=true | all-gather | bytes 18720 | tf_op jit(solution)/shard_map/all_gather | solution.py:37
  355.0 0.7 broadcast_select_fusion.1
  355.6 3.1 gather_fusion.1
  358.7 5.2 %fusion.31 = bf16[6144,128]{1,0:T(8,128)(2,1)} fusion(bf16[48,128,128]{2,1,0:T(8,128)(2,1)S(1)} %gather_fusion.1, pred[6144]{0:T(1024)(128)(4,1)S(1)} %get-tuple-element.114, pred[6144]{0:T(1024)(128)(4,1)S(1)} %get-tuple-element.113), kind=kLoop, calls=%fused_computation.43 | loop fusion | flops 1572864 | bytes 3158016 | tf_op jit(solution)/shard_map/jit(_where)/select_n | solution.py:178
  (105 shorter events, 6.5 us)
Async XLA Ops:
  7.2 4.8 %copy-start = (bf16[512,512]{1,0:T(8,128)(2,1)S(1)}, bf16[512,512]{1,0:T(8,128)(2,1)}, u32[]{:S(2)}) copy-start(bf16[512,512]{1,0:T(8,128)(2,1)} %param.10) | copy-start | bytes 1572868
  7.2 4.8 %copy-start.2 = (bf16[6144,512]{1,0:T(8,128)(2,1)S(1)}, bf16[6144,512]{1,0:T(8,128)(2,1)}, u32[]{:S(2)}) copy-start(bf16[6144,512]{1,0:T(8,128)(2,1)} %param.9) | copy-start | bytes 18874372
  20.0 3.7 copy-start.3
  28.9 2.8 copy-start.4
  31.7 2.8 copy-start.6
  31.7 2.8 copy-start.7
  117.8 10.0 %all-to-all-start = ((f32[4,1,12288]{2,1,0:T(1,128)}), f32[4,1,12288]{2,1,0:T(1,128)S(1)}, u32[]{:S(2)}, u32[]{:S(2)}) async-start(f32[4,1,12288]{2,1,0:T(1,128)} %broadcast_in_dim.174), calls=%async_computation | async-start | bytes 393216 | tf_op jit(solution)/shard_map/all_to_all | solution.py:16
  122.6 80.1 %all-gather.3.cloned.1.call-start = ((), (), s32[]{:S(2)}) async-start(), calls=%async_computation.2 | async-start | bytes 7864320 | tf_op jit(solution)/shard_map/all_gather | solution.py:101
  132.0 9.2 %copy-start.5 = (s32[1,24]{1,0:T(1,128)S(1)}, s32[1,24]{1,0:T(1,128)}, u32[]{:S(2)}) copy-start(s32[1,24]{1,0:T(1,128)} %param.13) | copy-start | bytes 292
  216.0 11.2 %copy-start.8 = (s32[1,24]{1,0:T(1,128)S(1)}, s32[1,24]{1,0:T(1,128)}, u32[]{:S(2)}) copy-start(s32[1,24]{1,0:T(1,128)} %param.14) | copy-start | bytes 292
  216.0 139.6 %all-to-all-start.1 = ((bf16[64,2,128,128]{3,2,1,0:T(8,128)(2,1)}), bf16[64,2,128,128]{3,2,1,0:T(8,128)(2,1)}, u32[]{:S(2)}, u32[]{:S(2)}) async-start(bf16[64,2,128,128]{3,2,1,0:T(8,128)(2,1)} %broadcast_select_fusion), calls=%async_computation.1 | async-start | bytes 8388608 | tf_op jit(solution)/shard_map/all_to_all | solution.py:174
  355.6 8.3 %copy-start.1 = (bf16[512,512]{1,0:T(8,128)(2,1)S(1)}, bf16[512,512]{1,0:T(8,128)(2,1)}, u32[]{:S(2)}) copy-start(bf16[512,512]{1,0:T(8,128)(2,1)} %param.10) | copy-start | bytes 1572868
Sparse Core Ops, SparseCore 0:
  132.1 70.5 all-gather.2
where the time goes:
time: 372 us; the launch traced here: 371 us
  blocking collectives  126 us (34%)
  waiting for transfers between devices  62.4 us (17%)
  matrix products  45 us (12%)
  loops' own time  37.9 us (10%)
  local copies, waits for them, and re-layouts  35.9 us (10%)
  other arithmetic  33.7 us (9%)
  starting transfers between devices  16 us (4%)
  between operations  14.3 us (4%)
    all_gather x1, blocking collectives, in_one_piece(): result = lax.all_gather(both, axis, axis=dim, tiled=True)  126 us
    all_gather x1, waiting for transfers between devices, layer_rows(): every_head = lax.all_gather(gated_rows, 'mp', axis=1, tiled=True)  60.7 us
    another operation x1, loops' own time, attend(): return lax.map(one_tile, tile_starts).reshape(row_count, head_size)  37.9 us
    dot_general x12, matrix products, one_tile(): return jnp.dot(weights, value_tile, preferred_element_type=jnp.float32)  31.4 us
    all_to_all x1, starting transfers between devices, per_device(): lax.all_to_all(outgoing, 'dp', split_axis=0, concat_axis=0, tiled=True)  11.2 us
    convert_element_type x1, other arithmetic, layer_rows(): widened = rows_in.astype(jnp.float32)  9.17 us
    unnamed x21, local copies, waits for them, and re-layouts  8.13 us
    dot_general x1, matrix products, layer_rows(): jnp.dot(normed, w_uvqk, preferred_element_type=jnp.float32)  7.98 us
  transfers between devices with their start and end apart: 3, of which 2 were waited for; matrix products, arithmetic and copies ran while one was open for 4% of the time, Pallas kernels for 0%

commit v1 on v0

--- a/solution.py
+++ b/solution.py
@@ -98,7 +98,8 @@
     gated_rows = ((outputs - average[:, None]) * lax.rsqrt(variance + EPS)[:, None] * gates).astype(
         jnp.bfloat16
     )
-    every_head = lax.all_gather(gated_rows, "mp", axis=1, tiled=True)
+    copies = jnp.concatenate([gated_rows] * lax.axis_size("mp"), axis=1)
+    every_head = lax.all_to_all(copies, "mp", 1, 1, tiled=True)
     out_columns = lax.dynamic_slice_in_dim(w_out, portion * quarter, quarter, 1)
     mixed_rows = jnp.dot(every_head, out_columns, preferred_element_type=jnp.float32)
     residual = lax.dynamic_slice_in_dim(widened, portion * quarter, quarter, 1)

time: 372 us -> 380 us (1.022)
  local copies, waits for them, and re-layouts: 35.9 us -> 50.9 us
  between operations: 14.3 us -> 0.96 us
  starting transfers between devices: 16 us -> 26 us
    all_gather x1 -> x0, waiting for transfers between devices: 60.7 us -> none  [layer_rows(): every_head = lax.all_gather(gated_rows, 'mp', axis=1, tiled=True)]
    all_to_all x0 -> x1, waiting for transfers between devices: none -> 58.4 us  [layer_rows(): every_head = lax.all_to_all(copies, 'mp', 1, 1, tiled=True)]
    all_to_all x0 -> x1, local copies, waits for them, and re-layouts: none -> 8.66 us  [layer_rows(): every_head = lax.all_to_all(copies, 'mp', 1, 1, tiled=True)]
    all_to_all x0 -> x1, starting transfers between devices: none -> 5.46 us  [layer_rows(): every_head = lax.all_to_all(copies, 'mp', 1, 1, tiled=True)]
    concatenate x0 -> x1, local copies, waits for them, and re-layouts: none -> 4.81 us  [layer_rows(): copies = jnp.concatenate([gated_rows] * lax.axis_size('mp'), axis=1)]
    all_to_all x1, starting transfers between devices: 11.2 us -> 15.7 us  [per_device(): lax.all_to_all(outgoing, 'dp', split_axis=0, concat_axis=0, tiled=True)]
where the time goes in v1:
time: 380 us; the launch traced here: 379 us
  blocking collectives  126 us (33%)
  waiting for transfers between devices  60.1 us (16%)
  local copies, waits for them, and re-layouts  50.9 us (13%)
  matrix products  45 us (12%)
  loops' own time  37.9 us (10%)
  other arithmetic  32.5 us (9%)
  starting transfers between devices  26 us (7%)
    all_gather x1, blocking collectives, in_one_piece(): result = lax.all_gather(both, axis, axis=dim, tiled=True)  126 us
    all_to_all x1, waiting for transfers between devices, layer_rows(): every_head = lax.all_to_all(copies, 'mp', 1, 1, tiled=True)  58.4 us
    another operation x1, loops' own time, attend(): return lax.map(one_tile, tile_starts).reshape(row_count, head_size)  37.9 us
    dot_general x12, matrix products, one_tile(): return jnp.dot(weights, value_tile, preferred_element_type=jnp.float32)  31.4 us
    all_to_all x1, starting transfers between devices, per_device(): lax.all_to_all(outgoing, 'dp', split_axis=0, concat_axis=0, tiled=True)  15.7 us
    convert_element_type x1, other arithmetic, layer_rows(): widened = rows_in.astype(jnp.float32)  9.17 us
    all_to_all x1, local copies, waits for them, and re-layouts, layer_rows(): every_head = lax.all_to_all(copies, 'mp', 1, 1, tiled=True)  8.66 us
    unnamed x21, local copies, waits for them, and re-layouts  8.14 us
  transfers between devices with their start and end apart: 3, of which 2 were waited for; matrix products, arithmetic and copies ran while one was open for 4% of the time, Pallas kernels for 0%

profile of v1, /device:TPU:1, one launch (start us, length us, event | category | flops | bytes accessed | tf_op | source)
XLA Modules:
  0.0 378.9 jit_solution(2022857201488740944)
XLA Ops:
  0.7 4.8 %convert_reduce_fusion = (f32[6144]{0:T(1024)S(1)}, f32[6144]{0:T(1024)S(1)}) fusion(bf16[6144,512]{1,0:T(8,128)(2,1)} %param.9), kind=kLoop, calls=%fused_computation.31 | loop fusion | flops 12570624 | bytes 6340608 | tf_op jit(solution)/shard_map/reduce_sum | solution.py:42
  5.5 8.0 %multiply_convert_fusion = bf16[6144,512]{0,1:T(8,128)(2,1)S(1)} fusion(bf16[512,512]{1,0:T(8,128)(2,1)S(1)} %copy-done, bf16[6144,512]{1,0:T(8,128)(2,1)S(1)} %copy-done.2, f32[6144]{0:T(1024)S(1)} %get-tuple-element.108, f32[6144]{0:T(1024)S(1)} %get-tuple-element.107), kind=kOutput, calls=%fused_computation.28 | convolution fusion | flops 3249537024 | bytes 13156352 | tf_op jit(solution)/shard_map/dot_general | solution.py:89
  13.5 2.3 fusion.59
  15.8 1.3 copy-done.3
  17.1 2.6 copy.65
  19.7 2.6 copy.66
  22.3 2.8 concatenate.21
  25.1 1.3 concatenate.22
  26.4 1.6 copy.64
  28.2 78.6 %while.11 = (s32[]{:T(128)}, f32[12,512,128]{2,1,0:T(8,128)}, s32[12]{0:T(128)S(1)}, s32[6144]{0:T(1024)S(1)}, s32[6272]{0:T(1024)S(1)}, /*index=5*/bf16[6144,12...) while((s32[]{:T(128)}, f32[12,512,128]{2,1,0:T(8,128)}, ...), condition=%wide.region_10.11_spmd.clone, body=%wide.region_9.10_spmd.clone.sunk | while | flops 171377152 | bytes 741060 | solution.py:77
  28.2 0.6 dynamic_slice.53
  32.1 2.6 fusion.70
  38.7 2.6 fusion.70
  45.2 2.6 fusion.70
  51.8 2.6 fusion.70
  54.4 0.6 dynamic_slice.53
  58.3 2.6 fusion.70
  64.9 2.6 fusion.70
  71.4 2.6 fusion.70
  74.0 0.6 dynamic_slice.53
  78.0 2.6 fusion.70
  80.6 0.6 dynamic_slice.53
  84.5 2.6 fusion.70
  87.1 0.6 dynamic_slice.53
  91.1 2.6 fusion.70
  93.7 0.6 dynamic_slice.53
  97.6 2.6 fusion.70
  104.2 2.6 fusion.70
  106.8 3.6 fusion.58
  110.4 0.8 broadcast_in_dim.174
  111.2 4.8 %all-to-all-start = ((f32[4,1,12288]{2,1,0:T(1,128)}), f32[4,1,12288]{2,1,0:T(1,128)S(1)}, u32[]{:S(2)}, u32[]{:S(2)}) async-start(f32[4,1,12288]{2,1,0:T(1,128)} %broadcast_in_dim.174), calls=%async_computation | async-start | bytes 393216 | tf_op jit(solution)/shard_map/all_to_all | solution.py:16
  116.0 3.5 copy.59
  119.6 1.6 all-to-all-done
  121.4 2.8 fusion.30
  124.3 1.6 copy.60
  125.8 4.8 %concatenate.24 = bf16[6144,4,128]{2,0,1:T(8,128)(2,1)} broadcast(bf16[6144,128]{1,0:T(8,128)(2,1)} %copy.60), dimensions={0,2} | broadcast | bytes 7864320 | tf_op jit(solution)/shard_map/concatenate | solution.py:101
  130.7 5.5 %all-to-all-start.1 = ((bf16[6144,4,128]{2,0,1:T(8,128)(2,1)}), bf16[6144,4,128]{2,0,1:T(8,128)(2,1)}, u32[]{:S(2)}, u32[]{:S(2)}) async-start(bf16[6144,4,128]{2,0,1:T(8,128)(2,1)} %concatenate.24), calls=%async_computation.1 | async-start | bytes 12582912 | tf_op jit(solution)/shard_map/all_to_all | solution.py:102
  136.1 9.2 %convert_element_type.38 = f32[6144,512]{1,0:T(8,128)} convert(bf16[6144,512]{1,0:T(8,128)(2,1)} %param.9) | non-fusion elementwise | flops 3145728 | bytes 18874368 | tf_op jit(solution)/shard_map/convert_element_type | solution.py:87
  146.1 58.4 %all-to-all-done.1 = bf16[6144,4,128]{2,0,1:T(8,128)(2,1)} async-done(((bf16[6144,4,128]{2,0,1:T(8,128)(2,1)}), bf16[6144,4,128]{2,0,1:T(8,128)(2,1)}, u32[]{:S(2)}, u32[]{:S(2)}) %all-to-all-start.1) | async-done | bytes 6291488 | tf_op jit(solution)/shard_map/all_to_all | solution.py:102
  204.5 8.7 %copy.61 = bf16[6144,4,128]{0,2,1:T(8,128)(2,1)} copy(bf16[6144,4,128]{2,0,1:T(8,128)(2,1)} %all-to-all-done.1) | data formatting | bytes 12582912 | tf_op jit(solution)/shard_map/all_to_all | solution.py:102
  213.2 5.6 %fusion.26 = bf16[6144,128]{1,0:T(8,128)(2,1)S(1)} fusion(bf16[6144,512]{0,1:T(8,128)(2,1)} %bitcast.65, f32[6144,512]{1,0:T(8,128)} %convert_element_type.38, s32[]{:T(128)S(6)} %select_n.164, bf16[512,512]{1,0:T(8,128)(2,1)} %param.11), kind=kOutput, calls=%fused_computation.33 | convolution fusion | flops 806879232 | bytes 11142144 | tf_op jit(solution)/shard_map/dot_general | solution.py:104
  218.8 3.1 gather_fusion
  221.9 4.6 %broadcast_select_fusion = bf16[64,2,128,128]{3,2,1,0:T(8,128)(2,1)} fusion(bf16[64,2,128,128]{3,2,1,0:T(8,128)(2,1)} %bitcast.67, pred[64,2]{1,0:T(8,128)(4,1)S(1)} %copy.54), kind=kLoop, calls=%fused_computation.37 | loop fusion | flops 2097152 | bytes 8388736 | tf_op jit(solution)/shard_map/jit(_take)/select_n | solution.py:174
  226.4 15.7 %all-to-all-start.2 = ((bf16[64,2,128,128]{3,2,1,0:T(8,128)(2,1)}), bf16[64,2,128,128]{3,2,1,0:T(8,128)(2,1)}, u32[]{:S(2)}, u32[]{:S(2)}) async-start(bf16[64,2,128,128]{3,2,1,0:T(8,128)(2,1)} %broadcast_select_fusion), calls=%async_computation.2 | async-start | bytes 8388608 | tf_op jit(solution)/shard_map/all_to_all | solution.py:175
  242.2 125.6 %all-gather = s32[64,1,72]{2,1,0:T(1,128)S(1)} all-gather(s32[1,1,72]{2,1,0:T(1,128)S(1)} %add_bitcast_fusion), channel_id=1, replica_groups=mesh['dp'=64,'mp'=4] {'dp'}, dimensions={0}, use_global_device_ids=true | all-gather | bytes 18720 | tf_op jit(solution)/shard_map/all_gather | solution.py:37
  369.9 0.7 broadcast_select_fusion.1
  370.6 3.1 gather_fusion.1
  373.7 5.2 %fusion.31 = bf16[6144,128]{1,0:T(8,128)(2,1)} fusion(bf16[48,128,128]{2,1,0:T(8,128)(2,1)S(1)} %gather_fusion.1, pred[6144]{0:T(1024)(128)(4,1)S(1)} %get-tuple-element.114, pred[6144]{0:T(1024)(128)(4,1)S(1)} %get-tuple-element.113), kind=kLoop, calls=%fused_computation.43 | loop fusion | flops 1572864 | bytes 3158016 | tf_op jit(solution)/shard_map/jit(_where)/select_n | solution.py:179
  (107 shorter events, 9.0 us)
Async XLA Ops:
  0.6 4.8 %copy-start = (bf16[512,512]{1,0:T(8,128)(2,1)S(1)}, bf16[512,512]{1,0:T(8,128)(2,1)}, u32[]{:S(2)}) copy-start(bf16[512,512]{1,0:T(8,128)(2,1)} %param.10) | copy-start | bytes 1572868
  0.7 4.8 %copy-start.2 = (bf16[6144,512]{1,0:T(8,128)(2,1)S(1)}, bf16[6144,512]{1,0:T(8,128)(2,1)}, u32[]{:S(2)}) copy-start(bf16[6144,512]{1,0:T(8,128)(2,1)} %param.9) | copy-start | bytes 18874372
  13.5 3.6 copy-start.3
  22.3 2.8 copy-start.4
  25.1 2.8 copy-start.6
  25.1 2.8 copy-start.7
  111.2 10.0 %all-to-all-start = ((f32[4,1,12288]{2,1,0:T(1,128)}), f32[4,1,12288]{2,1,0:T(1,128)S(1)}, u32[]{:S(2)}, u32[]{:S(2)}) async-start(f32[4,1,12288]{2,1,0:T(1,128)} %broadcast_in_dim.174), calls=%async_computation | async-start | bytes 393216 | tf_op jit(solution)/shard_map/all_to_all | solution.py:16
  130.7 73.9 %all-to-all-start.1 = ((bf16[6144,4,128]{2,0,1:T(8,128)(2,1)}), bf16[6144,4,128]{2,0,1:T(8,128)(2,1)}, u32[]{:S(2)}, u32[]{:S(2)}) async-start(bf16[6144,4,128]{2,0,1:T(8,128)(2,1)} %concatenate.24), calls=%async_computation.1 | async-start | bytes 12582912 | tf_op jit(solution)/shard_map/all_to_all | solution.py:102
  136.1 9.2 %copy-start.5 = (s32[1,24]{1,0:T(1,128)S(1)}, s32[1,24]{1,0:T(1,128)}, u32[]{:S(2)}) copy-start(s32[1,24]{1,0:T(1,128)} %param.13) | copy-start | bytes 292
  226.4 15.7 %copy-start.8 = (s32[1,24]{1,0:T(1,128)S(1)}, s32[1,24]{1,0:T(1,128)}, u32[]{:S(2)}) copy-start(s32[1,24]{1,0:T(1,128)} %param.14) | copy-start | bytes 292
  226.4 144.2 %all-to-all-start.2 = ((bf16[64,2,128,128]{3,2,1,0:T(8,128)(2,1)}), bf16[64,2,128,128]{3,2,1,0:T(8,128)(2,1)}, u32[]{:S(2)}, u32[]{:S(2)}) async-start(bf16[64,2,128,128]{3,2,1,0:T(8,128)(2,1)} %broadcast_select_fusion), calls=%async_computation.2 | async-start | bytes 8388608 | tf_op jit(solution)/shard_map/all_to_all | solution.py:175
  370.6 8.3 %copy-start.1 = (bf16[512,512]{1,0:T(8,128)(2,1)S(1)}, bf16[512,512]{1,0:T(8,128)(2,1)}, u32[]{:S(2)}) copy-start(bf16[512,512]{1,0:T(8,128)(2,1)} %param.10) | copy-start | bytes 1572868
